TPU v7x, 256 devices: a whole 4x4x8 slice. The times are simulated.
256 devices in a mesh: expert: 8 (over x, core), ffn: 32 (over z, y).
Axes of the slice: x: 4, y: 4, z: 8, core: 2. Of those that a mesh axis runs over, the one named last changes fastest.
Arguments:
- tokens: bfloat16 [8, 128, 4096], P('expert', 'ffn'), may hold values from -6 to 6
- routes: int32 [8, 128, 2], P('expert'), may hold values from 0 to 7, all different within a row; in each aligned block of 128 rows (0 to 127, 128 to 255, ..., all dimensions but the last counted through in order) at most 48 rows name the same one
- router: bfloat16 [4096, 8], replicated, may hold values from -0.09375 to 0.09375
- w_gate: bfloat16 [8, 4096, 12288], P('expert', None, 'ffn'), may hold values from -0.09375 to 0.09375
- w_up: bfloat16 [8, 4096, 12288], P('expert', None, 'ffn'), may hold values from -0.09375 to 0.09375
- w_down: bfloat16 [8, 12288, 4096], P('expert', 'ffn'), may hold values from -0.109375 to 0.109375
- adapter: bfloat16 [8, 4096, 4096], P('expert', None, 'ffn'), may hold values from -0.09375 to 0.09375
- upstream: bfloat16 [8, 128, 4096], P('expert', None, 'ffn'), may hold values from -24 to 24
- bound: float32 [8], P('expert'), may hold values from 2048 to 16384
Outputs:
- adapted: bfloat16 [8, 128, 4096], P('expert', None, 'ffn')
- clipped: bfloat16 [8, 4096, 4096], P('expert', None, 'ffn')
Inputs may be any that keep to these rules, and one draw needn't show every extreme that they name: `routes`: each token names two different experts; for each client at most 48 of its tokens name any one expert, and in some clients some expert is named by exactly 48 tokens.
All inputs are finite; a program needn't handle non-finite values.
Results may differ from a plain program's by a relative error of at most 0.015.
Values may be sent and summed in bfloat16 or wider, within the bound.
A program may use at most 64 MiB of HBM per device.

v0:
```python
import jax
import jax.numpy as jnp
from jax import lax
from jax.sharding import Mesh
from jax.sharding import PartitionSpec as P

FFN = ("ffn_0", "ffn_1")


def gathered_by_axis(value, axes, dim):
    out = value
    for number in range(len(axes) - 1, -1, -1):
        out = lax.all_gather(out, axes[number], axis=dim, tiled=True)
    return out


def own_rows(terms, axes):
    running = terms.astype(jnp.bfloat16)
    for axis in axes:
        running = lax.psum_scatter(running, axis, scatter_dimension=0, tiled=True)
    return running.astype(jnp.float32)


def in_order(parts, dim):
    dims = list(parts.shape[1:])
    dims[dim] *= parts.shape[0]
    return jnp.moveaxis(parts, 0, dim).reshape(dims)


def from_everyone(value, axis):
    copies = jnp.broadcast_to(value, (lax.axis_size(axis), *value.shape))
    return lax.all_to_all(copies, axis, split_axis=0, concat_axis=0, tiled=True)


def gathered_copies(value, axis, dim):
    return in_order(from_everyone(value, axis), dim)


def of_everyone(value, axis):
    everything = from_everyone(value, axis)
    return jnp.sum(everything, axis=0)


def slot_table(routed, expert_count):
    named_hits = jnp.sum(
        (routed[:, :, None] == jnp.arange(expert_count, dtype=jnp.int32)[None, None, :]).astype(
            jnp.int32
        ),
        axis=1,
    )
    before = jnp.cumsum(named_hits, axis=0) - named_hits
    return jnp.take_along_axis(before, routed, axis=1)


def pack_rows(token_rows, routed, expert_count, capacity):
    token_count = token_rows.shape[0]
    slot_flat = routed * capacity + slot_table(routed, expert_count)
    owners = jnp.repeat(jnp.arange(token_count, dtype=jnp.int32), 2)
    source = (
        jnp.full((expert_count * capacity,), token_count, jnp.int32)
        .at[slot_flat.reshape(-1)]
        .set(owners)
    )
    padded = jnp.concatenate(
        [token_rows, jnp.zeros((1, token_rows.shape[1]), token_rows.dtype)], axis=0
    )
    return (padded[source].reshape(expert_count, capacity, token_rows.shape[1]), slot_flat)


def mix_weights(token_rows, routed, router):
    logits = jnp.dot(token_rows, router, preferred_element_type=jnp.float32)
    picked = jnp.take_along_axis(logits, routed, axis=1)
    weight_first = jax.nn.sigmoid(picked[:, 0] - picked[:, 1])
    return (weight_first, 1.0 - weight_first)


def per_device(tokens, routes, router, w_gate, w_up, w_down, adapter, upstream, bound):
    expert_count = lax.axis_size("expert")
    gathered = gathered_by_axis(tokens, FFN, 1)
    token_rows = gathered[0]
    token_count = token_rows.shape[0]
    model_width = token_rows.shape[1]
    capacity = 3 * token_count // expert_count
    routed = routes[0]
    outgoing, slot_flat = pack_rows(token_rows, routed, expert_count, capacity)
    col_count = adapter.shape[2]
    column = lax.axis_index(FFN) * col_count
    weight_first, weight_second = mix_weights(token_rows, routed, router)
    arrived = lax.all_to_all(outgoing, "expert", split_axis=0, concat_axis=0, tiled=True)
    flat_rows = arrived.reshape(-1, model_width)
    gate_out = jnp.dot(flat_rows, w_gate[0], preferred_element_type=jnp.float32)
    up_out = jnp.dot(flat_rows, w_up[0], preferred_element_type=jnp.float32)
    hidden = (jax.nn.silu(gate_out) * up_out).astype(jnp.bfloat16)
    senders = arrived.shape[0]
    slots_here = arrived.shape[1]
    down_cols = w_down[0]
    term = lax.dot_general(
        down_cols, hidden, (((0,), (1,)), ((), ())), preferred_element_type=jnp.float32
    ).astype(jnp.bfloat16)
    term = lax.optimization_barrier(term).astype(jnp.float32)
    share = own_rows(
        jnp.transpose(term.reshape(col_count * lax.axis_size(FFN), senders, slots_here), (0, 2, 1)),
        FFN,
    )
    returned = lax.all_to_all(share, "expert", split_axis=2, concat_axis=2, tiled=True)
    slot_major = jnp.transpose(returned, (0, 2, 1)).reshape(col_count, -1)
    picked = slot_major[:, slot_flat]
    mix_cols = weight_first[None, :] * picked[:, :, 0] + weight_second[None, :] * picked[:, :, 1]
    own_tokens = lax.dynamic_slice_in_dim(token_rows, column, col_count, 1)
    own_layer = (own_tokens.astype(jnp.float32) + jnp.transpose(mix_cols)).astype(jnp.bfloat16)
    layer_out = gathered_copies(own_layer, FFN, 1)
    own_cols = lax.dynamic_slice_in_dim(layer_out, column, col_count, 1)
    adapted = (
        own_cols.astype(jnp.float32)
        + jnp.dot(layer_out, adapter[0], preferred_element_type=jnp.float32)
    ).astype(jnp.bfloat16)
    grad_input = upstream[0]
    adapter_grad = lax.dot_general(
        layer_out, grad_input, (((0,), (0,)), ((), ())), preferred_element_type=jnp.float32
    )
    squared = of_everyone(jnp.sum(adapter_grad * adapter_grad), FFN)
    grad_norm = jnp.sqrt(squared)
    clip_limit = bound[0]
    factor = clip_limit / jnp.maximum(grad_norm, clip_limit)
    clipped = (adapter_grad * factor).astype(jnp.bfloat16)
    return (adapted[None], clipped[None])


def solution(mesh):
    split = Mesh(mesh.devices.reshape(mesh.shape["expert"], 8, 4), ("expert", "ffn_0", "ffn_1"))
    placed = (
        P("expert", FFN, None),
        P("expert", None, None),
        P(),
        P("expert", None, FFN),
        P("expert", None, FFN),
        P("expert", FFN, None),
        P("expert", None, FFN),
        P("expert", None, FFN),
        P("expert"),
    )
    return jax.shard_map(
        per_device,
        mesh=split,
        in_specs=placed,
        out_specs=(P("expert", None, FFN), P("expert", None, FFN)),
        check_vma=False,
    )
```

profile of v0, /device:TPU:2, one launch (start us, length us, event | category | flops | bytes accessed | tf_op | source)
XLA Modules:
  0.0 286.1 jit_solution(3763902621592552826)
XLA Ops:
  7.2 1.0 copy.48
  8.2 12.8 %all_gather.6 = bf16[1,16,4096]{2,0,1:T(2,128)(2,1)S(1)} all-gather(bf16[1,4,4096]{2,0,1:T(2,128)(2,1)S(1)} %copy.48), channel_id=1, replica_groups=mesh['expert'=8,'ffn_0'=8,'ffn_1'=4] {'ffn_1'}, dimensions={1}, use_global_device_ids=true | all-gather | bytes 163840 | tf_op jit(solution)/shard_map/all_gather | solution.py:13
  21.0 0.8 copy.49
  21.8 0.8 copy.50
  22.6 0.7 convert_reduce_fusion
  23.3 0.1 copy.53
  23.4 0.1 squeeze.39
  23.6 0.1 reshape.235
  23.7 0.2 reduce_window_sum.11
  23.9 0.1 reshape.251
  24.1 1.9 gather_fusion.3
  26.0 1.4 scatter_custom_fusion
  27.5 35.2 %all-gather.2.cloned.1.call-done = bf16[1,128,4096]{2,1,0:T(8,128)(2,1)} async-done(((bf16[1,16,4096]{2,1,0:T(8,128)(2,1)}), bf16[1,128,4096]{2,1,0:T(8,128)(2,1)}) %all-gather.2.cloned.1.call-update) | async-done | bytes 1048592 | tf_op jit(solution)/shard_map/all_gather | solution.py:13
  62.7 2.3 concatenate.3
  65.0 9.7 %gather_fusion = bf16[384,4096]{1,0:T(8,128)(2,1)} fusion(bf16[129,4096]{1,0:T(8,128)(2,1)} %concatenate.3, s32[1024]{0:T(1024)S(1)} %pad_clamp_fusion.1), kind=kCustom, calls=%fused_computation | custom fusion | bytes 6292992 | tf_op jit(solution)/shard_map/gather | solution.py:67
  74.7 42.4 %all_to_all.21 = bf16[8,48,4096]{2,1,0:T(8,128)(2,1)S(1)} all-to-all(bf16[8,48,4096]{2,1,0:T(8,128)(2,1)} %bitcast.118), channel_id=1, replica_groups=mesh['expert'=8,'ffn_0'=8,'ffn_1'=4] {'expert'}, dimensions={0} | all-to-all | bytes 6291456 | tf_op jit(solution)/shard_map/all_to_all | solution.py:89
  117.1 1.7 copy-done.1
  118.8 2.6 fusion.4
  121.4 8.1 %fusion = bf16[4096,384]{0,1:T(8,128)(2,1)} fusion(bf16[1,384,4096]{2,1,0:T(8,128)(2,1)S(1)} %copy-done, bf16[384,4096]{1,0:T(8,128)(2,1)} %bitcast.124, bf16[1,4096,384]{2,1,0:T(8,128)(2,1)} %param.13, f32[384,384]{1,0:T(8,128)} %fusion.4), kind=kOutput, calls=%fused_computation.6 | convolution fusion | flops 2418376704 | bytes 13172736 | tf_op jit(solution)/shard_map/dot_general | solution.py:97
  129.5 0.2 reduce-scatter.7.cloned.1.call-start
  129.8 0.1 gather.22
  129.9 44.0 %reduce-scatter.5.cloned.1.call-done = bf16[512,48,8]{0,1,2:T(8,128)(2,1)} async-done(((bf16[4096,48,8]{0,1,2:T(8,128)(2,1)}), bf16[512,48,8]{0,1,2:T(8,128)(2,1)}) %reduce-scatter.5.cloned.1.call-update) | async-done | bytes 393232 | tf_op jit(solution)/shard_map/reduce_scatter | solution.py:20
  173.9 2.7 copy.58
  176.6 2.6 reshape.259
  179.3 0.1 reshape.229
  179.4 1.6 fusion.36
  181.0 1.4 gather_fusion.2
  182.4 0.1 reshape.238
  182.6 0.1 copy.51
  182.6 19.9 %reduce-scatter.7.cloned.1.call-done = bf16[128,384]{1,0:T(8,128)(2,1)} async-done(((bf16[512,384]{1,0:T(8,128)(2,1)}), bf16[128,384]{1,0:T(8,128)(2,1)}) %reduce-scatter.7.cloned.1.call-update) | async-done | bytes 98320
  202.5 1.1 reshape.260
  203.7 0.8 copy.59
  204.5 1.6 convert_element_type.49
  206.0 4.8 %all-to-all-start.1 = ((f32[128,48,8]{0,1,2:T(8,128)}), f32[128,48,8]{0,1,2:T(8,128)S(1)}, u32[]{:S(2)}, u32[]{:S(2)}) async-start(f32[128,48,8]{0,1,2:T(8,128)} %convert_element_type.49), calls=%async_computation.2 | async-start | bytes 393216 | tf_op jit(solution)/shard_map/all_to_all | solution.py:105
  210.8 5.3 %all-to-all-done.1 = f32[128,48,8]{0,1,2:T(8,128)S(1)} async-done(((f32[128,48,8]{0,1,2:T(8,128)}), f32[128,48,8]{0,1,2:T(8,128)S(1)}, u32[]{:S(2)}, u32[]{:S(2)}) %all-to-all-start.1) | async-done | bytes 196640 | tf_op jit(solution)/shard_map/all_to_all | solution.py:105
  216.2 0.7 gather_fusion.1
  216.9 0.9 fusion.28
  217.8 1.2 broadcast_in_dim.43
  219.0 8.4 %all-to-all-start.2 = ((bf16[32,128,128]{2,1,0:T(8,128)(2,1)}), bf16[32,128,128]{2,1,0:T(8,128)(2,1)}, u32[]{:S(2)}, u32[]{:S(2)}) async-start(bf16[32,128,128]{2,1,0:T(8,128)(2,1)} %broadcast_in_dim.43), calls=%async_computation.3 | async-start | bytes 2097152 | tf_op jit(solution)/shard_map/all_to_all | solution.py:32
  228.1 27.1 %all-to-all-done.2 = bf16[32,128,128]{2,1,0:T(8,128)(2,1)} async-done(((bf16[32,128,128]{2,1,0:T(8,128)(2,1)}), bf16[32,128,128]{2,1,0:T(8,128)(2,1)}, u32[]{:S(2)}, u32[]{:S(2)}) %all-to-all-start.2) | async-done | bytes 1048608 | tf_op jit(solution)/shard_map/all_to_all | solution.py:32
  255.2 3.8 %multiply_reduce_fusion = (f32[]{:T(128)}, f32[4096,128]{1,0:T(8,128)}) fusion(bf16[1,128,128]{2,1,0:T(8,128)(2,1)S(1)} %copy-done.3, bf16[32,128,128]{2,1,0:T(8,128)(2,1)} %all-to-all-done.2), kind=kOutput, calls=%fused_computation.13 | convolution fusion | flops 135266304 | bytes 3178500 | tf_op jit(solution)/shard_map/dot_general | solution.py:118
  259.0 1.3 broadcast_in_dim.45
  260.2 5.6 %all-to-all-start.3 = ((f32[32,1,1]{2,1,0:T(1,128)}), f32[32,1,1]{2,1,0:T(1,128)S(1)}, u32[]{:S(2)}, u32[]{:S(2)}) async-start(f32[32,1,1]{2,1,0:T(1,128)} %broadcast_in_dim.45), calls=%async_computation.4 | async-start | bytes 32768 | tf_op jit(solution)/shard_map/all_to_all | solution.py:32
  265.8 1.4 copy_bitcast_fusion
  267.2 2.3 fusion.13
  269.5 6.0 %all-to-all-done.3 = f32[32,1,1]{2,1,0:T(1,128)S(1)} async-done(((f32[32,1,1]{2,1,0:T(1,128)}), f32[32,1,1]{2,1,0:T(1,128)S(1)}, u32[]{:S(2)}, u32[]{:S(2)}) %all-to-all-start.3) | async-done | bytes 160 | tf_op jit(solution)/shard_map/all_to_all | solution.py:32
  275.5 0.6 reduce_sum.29
  276.9 2.7 fusion.14
  (27 shorter events, 0.3 us)
Async XLA Ops:
  7.2 114.2 %copy-start = (bf16[1,384,4096]{2,1,0:T(8,128)(2,1)S(1)}, bf16[1,384,4096]{2,1,0:T(8,128)(2,1)}, u32[]{:S(2)}) copy-start(bf16[1,384,4096]{2,1,0:T(8,128)(2,1)} %param.14) | copy-start | bytes 9437188
  7.2 55.5 %all-gather.2.cloned.1.call-start = ((), (), s32[]{:S(2)}) async-start(), calls=%async_computation.6 | async-start | bytes 1179648 | tf_op jit(solution)/shard_map/all_gather | solution.py:13
  21.8 152.1 %reduce-scatter.5.cloned.1.call-start = ((), (), s32[]{:S(2)}) async-start(), calls=%async_computation.7 | async-start | bytes 3538944 | tf_op jit(solution)/shard_map/reduce_scatter | solution.py:20
  74.7 44.1 %copy-start.5 = (bf16[1,4096,384]{2,1,0:T(8,128)(2,1)S(1)}, bf16[1,4096,384]{2,1,0:T(8,128)(2,1)}, u32[]{:S(2)}) copy-start(bf16[1,4096,384]{2,1,0:T(8,128)(2,1)} %param.12) | copy-start | bytes 9437188
  117.1 1.7 copy-start.1
  129.5 49.9 %copy-start.2 = (bf16[4096,8]{0,1:T(8,128)(2,1)S(1)}, bf16[4096,8]{0,1:T(8,128)(2,1)}, u32[]{:S(2)}) copy-start(bf16[4096,8]{0,1:T(8,128)(2,1)} %param.11) | copy-start | bytes 196612
  129.5 73.0 %reduce-scatter.7.cloned.1.call-start = ((), (), s32[]{:S(2)}) async-start(), calls=%async_computation.8 | async-start | bytes 491520
  181.0 1.6 copy-start.4
  206.0 10.1 %all-to-all-start.1 = ((f32[128,48,8]{0,1,2:T(8,128)}), f32[128,48,8]{0,1,2:T(8,128)S(1)}, u32[]{:S(2)}, u32[]{:S(2)}) async-start(f32[128,48,8]{0,1,2:T(8,128)} %convert_element_type.49), calls=%async_computation.2 | async-start | bytes 393216 | tf_op jit(solution)/shard_map/all_to_all | solution.py:105
  216.9 38.3 %copy-start.3 = (bf16[1,128,128]{2,1,0:T(8,128)(2,1)S(1)}, bf16[1,128,128]{2,1,0:T(8,128)(2,1)}, u32[]{:S(2)}) copy-start(bf16[1,128,128]{2,1,0:T(8,128)(2,1)} %param.16) | copy-start | bytes 98308
  219.0 36.2 %all-to-all-start.2 = ((bf16[32,128,128]{2,1,0:T(8,128)(2,1)}), bf16[32,128,128]{2,1,0:T(8,128)(2,1)}, u32[]{:S(2)}, u32[]{:S(2)}) async-start(bf16[32,128,128]{2,1,0:T(8,128)(2,1)} %broadcast_in_dim.43), calls=%async_computation.3 | async-start | bytes 2097152 | tf_op jit(solution)/shard_map/all_to_all | solution.py:32
  260.2 15.3 %all-to-all-start.3 = ((f32[32,1,1]{2,1,0:T(1,128)}), f32[32,1,1]{2,1,0:T(1,128)S(1)}, u32[]{:S(2)}, u32[]{:S(2)}) async-start(f32[32,1,1]{2,1,0:T(1,128)} %broadcast_in_dim.45), calls=%async_computation.4 | async-start | bytes 32768 | tf_op jit(solution)/shard_map/all_to_all | solution.py:32
Sparse Core Ops, SparseCore 0:
  21.9 40.6 all-gather.1
  129.6 44.1 reduce-scatter.4
  179.3 23.1 reduce-scatter.6
where the time goes:
time: 287 us; the launch traced here: 286 us
  waiting for transfers between devices  138 us (48%)
  blocking collectives  55.2 us (19%)
  local copies, waits for them, and re-layouts  33.8 us (12%)
  starting transfers between devices  19.1 us (7%)
  matrix products  18.4 us (6%)
  between operations  15.3 us (5%)
  other arithmetic  6.74 us (2%)
    reduce_scatter x1, waiting for transfers between devices, own_rows(): running = lax.psum_scatter(running, axis, scatter_dimension=0, tiled=True)  44 us
    all_to_all x1, blocking collectives, per_device(): lax.all_to_all(outgoing, 'expert', split_axis=0, concat_axis=0, tiled=True)  42.4 us
    all_gather x1, waiting for transfers between devices, gathered_by_axis(): out = lax.all_gather(out, axes[number], axis=dim, tiled=True)  35.2 us
    all_to_all x2, waiting for transfers between devices, from_everyone(): return lax.all_to_all(copies, axis, split_axis=0, concat_axis=0, tiled=True)  33.1 us
    unnamed x4, waiting for transfers between devices  19.9 us
    all_to_all x2, starting transfers between devices, from_everyone(): return lax.all_to_all(copies, axis, split_axis=0, concat_axis=0, tiled=True)  14 us
    all_gather x1, blocking collectives, gathered_by_axis(): out = lax.all_gather(out, axes[number], axis=dim, tiled=True)  12.8 us
    unnamed x18, local copies, waits for them, and re-layouts  10.7 us
  transfers between devices with their start and end apart: 6, of which 6 were waited for; matrix products, arithmetic and copies ran while one was open for 4% of the time, Pallas kernels for 0%

commit v1 on v0

--- a/solution.py
+++ b/solution.py
@@ -1,3 +1,4 @@
+import functools
 import jax
 import jax.numpy as jnp
 from jax import lax
@@ -5,6 +6,40 @@
 from jax.sharding import PartitionSpec as P
 
 FFN = ("ffn_0", "ffn_1")
+
+
+def group_the_state(original, axis_no, local_array):
+    f_now, value_now = (original.shape[:axis_no], original.shape[axis_no + 1 :])
+    right_arr = original.reshape(*f_now, local_array, -1, *value_now)
+    out_arr = jnp.moveaxis(right_arr, axis_no, 0)
+    return out_arr
+
+
+def sector_try_all(xs, in_dim):
+    xs = jnp.moveaxis(xs, 0, in_dim)
+    response = xs.shape
+    s_next = xs.reshape(
+        *response[:in_dim], response[in_dim] * response[in_dim + 1], *response[in_dim + 2 :]
+    )
+    return s_next
+
+
+def boxes_derive(point, lane_axis, message, m):
+    state_next = jax.lax.axis_size(lane_axis)
+    high, odd = (state_next, jax.lax.axis_index(lane_axis))
+    fresh = group_the_state(point, message, high)
+    made = [fresh[odd]]
+    for ii in tuple(range(1, high)):
+        x_now = fresh[(odd + ii) % high]
+        clean = jax.lax.ppermute(x_now, lane_axis, [(q, (q + ii) % high) for q in range(high)])
+        made.append(clean)
+    heard = jnp.stack(made)
+    fresh = heard[(odd - jnp.arange(high)) % high]
+    z = sector_try_all(fresh, m)
+    return z
+
+
+serve_edge = functools.partial(boxes_derive, lane_axis="expert", message=0, m=0)
 
 
 def gathered_by_axis(value, axes, dim):
@@ -86,7 +121,7 @@
     col_count = adapter.shape[2]
     column = lax.axis_index(FFN) * col_count
     weight_first, weight_second = mix_weights(token_rows, routed, router)
-    arrived = lax.all_to_all(outgoing, "expert", split_axis=0, concat_axis=0, tiled=True)
+    arrived = serve_edge(outgoing)
     flat_rows = arrived.reshape(-1, model_width)
     gate_out = jnp.dot(flat_rows, w_gate[0], preferred_element_type=jnp.float32)
     up_out = jnp.dot(flat_rows, w_up[0], preferred_element_type=jnp.float32)

time: 287 us -> 299 us (1.042)
  blocking collectives: 55.2 us -> 12.8 us
  waiting for transfers between devices: 138 us -> 170 us
  local copies, waits for them, and re-layouts: 33.8 us -> 44.6 us
  starting transfers between devices: 19.1 us -> 26.5 us
    all_to_all x1 -> x0, blocking collectives: 42.4 us -> none  [per_device(): lax.all_to_all(outgoing, 'expert', split_axis=0, concat_axis=0, tiled=True)]
    ppermute x0 -> x7, waiting for transfers between devices: none -> 29.5 us  [boxes_derive(): jax.lax.ppermute(x_now, lane_axis, [(q, (q + ii) % high) for q in range(h...]
    ppermute x0 -> x7, starting transfers between devices: none -> 7.61 us  [boxes_derive(): jax.lax.ppermute(x_now, lane_axis, [(q, (q + ii) % high) for q in range(h...]
    gather x0 -> x1, local copies, waits for them, and re-layouts: none -> 4.27 us  [boxes_derive(): fresh = heard[(odd - jnp.arange(high)) % high]]
    reduce_scatter x1, waiting for transfers between devices: 44 us -> 47.7 us  [own_rows(): running = lax.psum_scatter(running, axis, scatter_dimension=0, tiled=True)]
    unnamed x18 -> x20, local copies, waits for them, and re-layouts: 10.7 us -> 13.7 us
  transfers between devices with their start and end apart: 6 -> 13, of which waited for: 6 -> 9; matrix products, arithmetic and copies ran while one was open for 4% -> 6% of each run, Pallas kernels for 0% -> 0%
where the time goes in v1:
time: 299 us; the launch traced here: 298 us
  waiting for transfers between devices  170 us (57%)
  local copies, waits for them, and re-layouts  44.6 us (15%)
  starting transfers between devices  26.5 us (9%)
  matrix products  21.2 us (7%)
  between operations  15.5 us (5%)
  blocking collectives  12.8 us (4%)
  other arithmetic  6.76 us (2%)
    reduce_scatter x1, waiting for transfers between devices, own_rows(): running = lax.psum_scatter(running, axis, scatter_dimension=0, tiled=True)  47.7 us
    all_gather x1, waiting for transfers between devices, gathered_by_axis(): out = lax.all_gather(out, axes[number], axis=dim, tiled=True)  35 us
    all_to_all x2, waiting for transfers between devices, from_everyone(): return lax.all_to_all(copies, axis, split_axis=0, concat_axis=0, tiled=True)  33.1 us
    ppermute x7, waiting for transfers between devices, boxes_derive(): jax.lax.ppermute(x_now, lane_axis, [(q, (q + ii) % high) for q in range(h...  29.5 us
    unnamed x4, waiting for transfers between devices  19.8 us
    all_to_all x2, starting transfers between devices, from_everyone(): return lax.all_to_all(copies, axis, split_axis=0, concat_axis=0, tiled=True)  14 us
    unnamed x20, local copies, waits for them, and re-layouts  13.7 us
    all_gather x1, blocking collectives, gathered_by_axis(): out = lax.all_gather(out, axes[number], axis=dim, tiled=True)  12.8 us
  transfers between devices with their start and end apart: 13, of which 9 were waited for; matrix products, arithmetic and copies ran while one was open for 6% of the time, Pallas kernels for 0%

profile of v1, /device:TPU:2, one launch (start us, length us, event | category | flops | bytes accessed | tf_op | source)
XLA Modules:
  0.0 297.8 jit_solution(648970934692313867)
XLA Ops:
  7.2 1.0 copy.48
  8.2 12.8 %all_gather.6 = bf16[1,16,4096]{2,0,1:T(2,128)(2,1)S(1)} all-gather(bf16[1,4,4096]{2,0,1:T(2,128)(2,1)S(1)} %copy.48), channel_id=1, replica_groups=mesh['expert'=8,'ffn_0'=8,'ffn_1'=4] {'ffn_1'}, dimensions={1}, use_global_device_ids=true | all-gather | bytes 163840 | tf_op jit(solution)/shard_map/all_gather | solution.py:48
  21.0 0.8 copy.49
  21.9 0.8 copy.50
  24.2 1.9 gather_fusion.4
  26.2 1.4 scatter_custom_fusion
  27.6 35.0 %all-gather.2.cloned.1.call-done = bf16[1,128,4096]{2,1,0:T(8,128)(2,1)} async-done(((bf16[1,16,4096]{2,1,0:T(8,128)(2,1)}), bf16[1,128,4096]{2,1,0:T(8,128)(2,1)}) %all-gather.2.cloned.1.call-update) | async-done | bytes 1048592 | tf_op jit(solution)/shard_map/all_gather | solution.py:48
  62.7 2.4 concatenate.3
  65.0 9.6 %gather_fusion = bf16[384,4096]{1,0:T(8,128)(2,1)} fusion(bf16[129,4096]{1,0:T(8,128)(2,1)} %concatenate.3, s32[1024]{0:T(1024)S(1)} %pad_clamp_fusion.2), kind=kCustom, calls=%fused_computation | custom fusion | bytes 6292992 | tf_op jit(solution)/shard_map/gather | solution.py:102
  74.6 2.8 dynamic-slice_bitcast_fusion
  77.5 1.8 collective-permute-start.6
  79.2 1.8 collective-permute-start.5
  81.1 1.5 collective-permute-start.3
  82.6 2.6 collective-permute-done
  85.2 1.5 collective-permute-start.1
  86.6 0.8 bitcast_dynamic-update-slice_fusion.6
  87.4 18.3 %collective-permute-done.1 = bf16[1,48,4096]{2,1,0:T(8,128)(2,1)S(1)} collective-permute-done((bf16[1,48,4096]{2,1,0:T(8,128)(2,1)S(1)}, bf16[1,48,4096]{2,1,0:T(8,128)(2,1)S(1)}, u32[]{:S(2)}, u32[]{:S(2)}) %collective-permute-start.1) | collective-permute-done | bytes 393248 | tf_op jit(solution)/shard_map/ppermute | solution.py:34
  105.8 1.0 collective-permute-start.2
  107.6 8.5 %collective-permute-done.2 = bf16[1,48,4096]{2,1,0:T(8,128)(2,1)S(1)} collective-permute-done((bf16[1,48,4096]{2,1,0:T(8,128)(2,1)S(1)}, bf16[1,48,4096]{2,1,0:T(8,128)(2,1)S(1)}, u32[]{:S(2)}, u32[]{:S(2)}) %collective-permute-start.2) | collective-permute-done | bytes 393248 | tf_op jit(solution)/shard_map/ppermute | solution.py:34
  116.1 0.8 bitcast_dynamic-update-slice_fusion.4
  116.9 0.8 bitcast_dynamic-update-slice_fusion.3
  117.7 0.8 bitcast_dynamic-update-slice_fusion.2
  118.4 0.8 bitcast_dynamic-update-slice_fusion.1
  120.0 4.3 %gather_fusion.1 = bf16[8,48,4096]{2,1,0:T(8,128)(2,1)} fusion(bf16[8,48,4096]{2,1,0:T(8,128)(2,1)} %bitcast.22, s32[1024]{0:T(1024)S(1)} %pad_clamp_fusion.1), kind=kCustom, calls=%fused_computation.1 | custom fusion | bytes 6291488 | tf_op jit(solution)/shard_map/gather | solution.py:37
  124.3 5.4 %fusion.4 = f32[384,384]{1,0:T(8,128)} fusion(bf16[384,4096]{1,0:T(8,128)(2,1)} %bitcast.154, bf16[1,4096,384]{2,1,0:T(8,128)(2,1)} %param.12), kind=kOutput, calls=%fused_computation.11 | convolution fusion | flops 1207959552 | bytes 6881280 | tf_op jit(solution)/shard_map/dot_general | solution.py:126
  129.7 8.1 %fusion = bf16[4096,384]{0,1:T(8,128)(2,1)} fusion(bf16[1,384,4096]{2,1,0:T(8,128)(2,1)S(1)} %copy-done, bf16[384,4096]{1,0:T(8,128)(2,1)} %bitcast.155, bf16[1,4096,384]{2,1,0:T(8,128)(2,1)} %param.13, f32[384,384]{1,0:T(8,128)} %fusion.4), kind=kOutput, calls=%fused_computation.7 | convolution fusion | flops 2418376704 | bytes 13172736 | tf_op jit(solution)/shard_map/dot_general | solution.py:132
  138.0 47.7 %reduce-scatter.5.cloned.1.call-done = bf16[512,48,8]{0,1,2:T(8,128)(2,1)} async-done(((bf16[4096,48,8]{0,1,2:T(8,128)(2,1)}), bf16[512,48,8]{0,1,2:T(8,128)(2,1)}) %reduce-scatter.5.cloned.1.call-update) | async-done | bytes 393232 | tf_op jit(solution)/shard_map/reduce_scatter | solution.py:55
  185.7 2.7 copy.58
  188.4 2.6 reshape.311
  191.2 1.6 fusion.38
  192.8 1.4 gather_fusion.3
  194.4 19.8 %reduce-scatter.7.cloned.1.call-done = bf16[128,384]{1,0:T(8,128)(2,1)} async-done(((bf16[512,384]{1,0:T(8,128)(2,1)}), bf16[128,384]{1,0:T(8,128)(2,1)}) %reduce-scatter.7.cloned.1.call-update) | async-done | bytes 98320
  214.2 1.1 reshape.312
  215.4 0.8 copy.59
  216.2 1.6 convert_element_type.49
  217.8 4.8 %all-to-all-start = ((f32[128,48,8]{0,1,2:T(8,128)}), f32[128,48,8]{0,1,2:T(8,128)S(1)}, u32[]{:S(2)}, u32[]{:S(2)}) async-start(f32[128,48,8]{0,1,2:T(8,128)} %convert_element_type.49), calls=%async_computation.1 | async-start | bytes 393216 | tf_op jit(solution)/shard_map/all_to_all | solution.py:140
  222.6 5.3 %all-to-all-done = f32[128,48,8]{0,1,2:T(8,128)S(1)} async-done(((f32[128,48,8]{0,1,2:T(8,128)}), f32[128,48,8]{0,1,2:T(8,128)S(1)}, u32[]{:S(2)}, u32[]{:S(2)}) %all-to-all-start) | async-done | bytes 196640 | tf_op jit(solution)/shard_map/all_to_all | solution.py:140
  228.7 0.9 fusion.28
  229.5 1.2 broadcast_in_dim.44
  230.8 8.4 %all-to-all-start.1 = ((bf16[32,128,128]{2,1,0:T(8,128)(2,1)}), bf16[32,128,128]{2,1,0:T(8,128)(2,1)}, u32[]{:S(2)}, u32[]{:S(2)}) async-start(bf16[32,128,128]{2,1,0:T(8,128)(2,1)} %broadcast_in_dim.44), calls=%async_computation.2 | async-start | bytes 2097152 | tf_op jit(solution)/shard_map/all_to_all | solution.py:67
  239.8 27.1 %all-to-all-done.1 = bf16[32,128,128]{2,1,0:T(8,128)(2,1)} async-done(((bf16[32,128,128]{2,1,0:T(8,128)(2,1)}), bf16[32,128,128]{2,1,0:T(8,128)(2,1)}, u32[]{:S(2)}, u32[]{:S(2)}) %all-to-all-start.1) | async-done | bytes 1048608 | tf_op jit(solution)/shard_map/all_to_all | solution.py:67
  266.9 3.8 %multiply_reduce_fusion = (f32[]{:T(128)}, f32[4096,128]{1,0:T(8,128)}) fusion(bf16[1,128,128]{2,1,0:T(8,128)(2,1)S(1)} %copy-done.2, bf16[32,128,128]{2,1,0:T(8,128)(2,1)} %all-to-all-done.1), kind=kOutput, calls=%fused_computation.14 | convolution fusion | flops 135266304 | bytes 3178500 | tf_op jit(solution)/shard_map/dot_general | solution.py:153
  270.7 1.3 broadcast_in_dim.46
  272.0 5.6 %all-to-all-start.2 = ((f32[32,1,1]{2,1,0:T(1,128)}), f32[32,1,1]{2,1,0:T(1,128)S(1)}, u32[]{:S(2)}, u32[]{:S(2)}) async-start(f32[32,1,1]{2,1,0:T(1,128)} %broadcast_in_dim.46), calls=%async_computation.3 | async-start | bytes 32768 | tf_op jit(solution)/shard_map/all_to_all | solution.py:67
  277.6 1.4 copy_bitcast_fusion
  279.0 2.3 fusion.13
  281.2 6.0 %all-to-all-done.2 = f32[32,1,1]{2,1,0:T(1,128)S(1)} async-done(((f32[32,1,1]{2,1,0:T(1,128)}), f32[32,1,1]{2,1,0:T(1,128)S(1)}, u32[]{:S(2)}, u32[]{:S(2)}) %all-to-all-start.2) | async-done | bytes 160 | tf_op jit(solution)/shard_map/all_to_all | solution.py:67
  288.6 2.7 fusion.14
  (47 shorter events, 5.2 us)
Async XLA Ops:
  7.2 122.6 %copy-start = (bf16[1,384,4096]{2,1,0:T(8,128)(2,1)S(1)}, bf16[1,384,4096]{2,1,0:T(8,128)(2,1)}, u32[]{:S(2)}) copy-start(bf16[1,384,4096]{2,1,0:T(8,128)(2,1)} %param.14) | copy-start | bytes 9437188
  7.2 55.5 %all-gather.2.cloned.1.call-start = ((), (), s32[]{:S(2)}) async-start(), calls=%async_computation.5 | async-start | bytes 1179648 | tf_op jit(solution)/shard_map/all_gather | solution.py:48
  21.8 163.9 %reduce-scatter.5.cloned.1.call-start = ((), (), s32[]{:S(2)}) async-start(), calls=%async_computation.6 | async-start | bytes 3538944 | tf_op jit(solution)/shard_map/reduce_scatter | solution.py:55
  77.4 7.7 %collective-permute-start = (bf16[1,48,4096]{2,1,0:T(8,128)(2,1)S(1)}, bf16[1,48,4096]{2,1,0:T(8,128)(2,1)S(1)}, u32[]{:S(2)}, u32[]{:S(2)}) collective-permute-start(bf16[1,48,4096]{2,1,0:T(8,128)(2,1)S(1)} %get-tuple-element.10), channel_id=1, source_target_pairs={{0,32},{32,64},{64,96},{96,128},{128,160},{160,192},{192,224},{224... | collective-permute-start | bytes 1179656 | tf_op jit(solution)/shard_map/ppermute | solution.py:34
  77.5 41.8 %collective-permute-start.6 = (bf16[1,48,4096]{2,1,0:T(8,128)(2,1)S(1)}, bf16[1,48,4096]{2,1,0:T(8,128)(2,1)S(1)}, u32[]{:S(2)}, u32[]{:S(2)}) collective-permute-start(bf16[1,48,4096]{2,1,0:T(8,128)(2,1)S(1)} %get-tuple-element.4), channel_id=1, source_target_pairs={{0,224},{32,0},{64,32},{96,64},{128,96},{160,128},{192,160},{224,1... | collective-permute-start | bytes 1179656 | tf_op jit(solution)/shard_map/ppermute | solution.py:34
  79.2 39.2 %collective-permute-start.5 = (bf16[1,48,4096]{2,1,0:T(8,128)(2,1)S(1)}, bf16[1,48,4096]{2,1,0:T(8,128)(2,1)S(1)}, u32[]{:S(2)}, u32[]{:S(2)}) collective-permute-start(bf16[1,48,4096]{2,1,0:T(8,128)(2,1)S(1)} %get-tuple-element.5), channel_id=1, source_target_pairs={{0,192},{32,224},{64,0},{96,32},{128,64},{160,96},{192,128},{224,1... | collective-permute-start | bytes 1179656 | tf_op jit(solution)/shard_map/ppermute | solution.py:34
  81.0 36.7 %collective-permute-start.4 = (bf16[1,48,4096]{2,1,0:T(8,128)(2,1)S(1)}, bf16[1,48,4096]{2,1,0:T(8,128)(2,1)S(1)}, u32[]{:S(2)}, u32[]{:S(2)}) collective-permute-start(bf16[1,48,4096]{2,1,0:T(8,128)(2,1)S(1)} %get-tuple-element.6), channel_id=1, source_target_pairs={{0,160},{32,192},{64,224},{96,0},{128,32},{160,64},{192,96},{224,1... | collective-permute-start | bytes 1179656 | tf_op jit(solution)/shard_map/ppermute | solution.py:34
  81.1 35.7 %collective-permute-start.3 = (bf16[1,48,4096]{2,1,0:T(8,128)(2,1)S(1)}, bf16[1,48,4096]{2,1,0:T(8,128)(2,1)S(1)}, u32[]{:S(2)}, u32[]{:S(2)}) collective-permute-start(bf16[1,48,4096]{2,1,0:T(8,128)(2,1)S(1)} %get-tuple-element.7), channel_id=1, source_target_pairs={{0,128},{32,160},{64,192},{96,224},{128,0},{160,32},{192,64},{224,... | collective-permute-start | bytes 1179656 | tf_op jit(solution)/shard_map/ppermute | solution.py:34
  85.2 20.6 %collective-permute-start.1 = (bf16[1,48,4096]{2,1,0:T(8,128)(2,1)S(1)}, bf16[1,48,4096]{2,1,0:T(8,128)(2,1)S(1)}, u32[]{:S(2)}, u32[]{:S(2)}) collective-permute-start(bf16[1,48,4096]{2,1,0:T(8,128)(2,1)S(1)} %get-tuple-element.9), channel_id=1, source_target_pairs={{0,64},{32,96},{64,128},{96,160},{128,192},{160,224},{192,0},{224,... | collective-permute-start | bytes 1179656 | tf_op jit(solution)/shard_map/ppermute | solution.py:34
  105.8 10.3 %collective-permute-start.2 = (bf16[1,48,4096]{2,1,0:T(8,128)(2,1)S(1)}, bf16[1,48,4096]{2,1,0:T(8,128)(2,1)S(1)}, u32[]{:S(2)}, u32[]{:S(2)}) collective-permute-start(bf16[1,48,4096]{2,1,0:T(8,128)(2,1)S(1)} %get-tuple-element.8), channel_id=1, source_target_pairs={{0,96},{32,128},{64,160},{96,192},{128,224},{160,0},{192,32},{224,... | collective-permute-start | bytes 1179656 | tf_op jit(solution)/shard_map/ppermute | solution.py:34
  137.8 53.4 %copy-start.1 = (bf16[4096,8]{0,1:T(8,128)(2,1)S(1)}, bf16[4096,8]{0,1:T(8,128)(2,1)}, u32[]{:S(2)}) copy-start(bf16[4096,8]{0,1:T(8,128)(2,1)} %param.11) | copy-start | bytes 196612
  137.8 76.4 %reduce-scatter.7.cloned.1.call-start = ((), (), s32[]{:S(2)}) async-start(), calls=%async_computation.7 | async-start | bytes 491520
  192.8 1.6 copy-start.3
  217.8 10.2 %all-to-all-start = ((f32[128,48,8]{0,1,2:T(8,128)}), f32[128,48,8]{0,1,2:T(8,128)S(1)}, u32[]{:S(2)}, u32[]{:S(2)}) async-start(f32[128,48,8]{0,1,2:T(8,128)} %convert_element_type.49), calls=%async_computation.1 | async-start | bytes 393216 | tf_op jit(solution)/shard_map/all_to_all | solution.py:140
  228.6 38.3 %copy-start.2 = (bf16[1,128,128]{2,1,0:T(8,128)(2,1)S(1)}, bf16[1,128,128]{2,1,0:T(8,128)(2,1)}, u32[]{:S(2)}) copy-start(bf16[1,128,128]{2,1,0:T(8,128)(2,1)} %param.16) | copy-start | bytes 98308
  230.8 36.2 %all-to-all-start.1 = ((bf16[32,128,128]{2,1,0:T(8,128)(2,1)}), bf16[32,128,128]{2,1,0:T(8,128)(2,1)}, u32[]{:S(2)}, u32[]{:S(2)}) async-start(bf16[32,128,128]{2,1,0:T(8,128)(2,1)} %broadcast_in_dim.44), calls=%async_computation.2 | async-start | bytes 2097152 | tf_op jit(solution)/shard_map/all_to_all | solution.py:67
  272.0 15.3 %all-to-all-start.2 = ((f32[32,1,1]{2,1,0:T(1,128)}), f32[32,1,1]{2,1,0:T(1,128)S(1)}, u32[]{:S(2)}, u32[]{:S(2)}) async-start(f32[32,1,1]{2,1,0:T(1,128)} %broadcast_in_dim.46), calls=%async_computation.3 | async-start | bytes 32768 | tf_op jit(solution)/shard_map/all_to_all | solution.py:67
Sparse Core Ops, SparseCore 0:
  21.9 40.6 all-gather.1
  137.9 47.6 reduce-scatter.4
  191.1 23.0 reduce-scatter.6
